TPU v7x, 32 devices: a whole 2x2x4 slice. The times are simulated.
32 devices in a mesh: grp: 2 (over y), gx: 16 (over z, x, core), gy: 1.
Axes of the slice: x: 2, y: 2, z: 4, core: 2. Of those that a mesh axis runs over, the one named last changes fastest.
Arguments:
- residue_feats: bfloat16 [512, 256], P(('grp', 'gx')), parts along dimension 0, may hold values from -6 to 6
- pair_feats: bfloat16 [64, 512, 256], P(None, ('grp', 'gx'), 'gy'), parts along dimension 1, may hold values from -30 to 30
- w_row: bfloat16 [256, 64], replicated, may hold values from -0.375 to 0.375
- w_col: bfloat16 [256, 64], replicated, may hold values from -0.375 to 0.375
- first_taps: bfloat16 [9, 64, 64], replicated, may hold values from -0.25 to 0.25
- second_taps: bfloat16 [9, 64, 64], replicated, may hold values from -0.25 to 0.25
- norm_scale: float32 [2, 64], replicated, may hold values from 0.25 to 1.75
- norm_shift: float32 [2, 64], replicated, may hold values from -2 to 2
Outputs:
- symmetric: bfloat16 [64, 512, 256], P(None, ('grp', 'gx'), 'gy'), parts along dimension 1
There are 2 independent parts, one for each index of `grp`. A program takes and returns all parts, laid end to end along the dimension named above; an argument that names none is the same for every part. Nothing has to cross between parts.
All inputs are finite; a program needn't handle non-finite values.
Results may differ from a plain program's by a relative error of at most 0.012.
Values may be sent and summed in bfloat16 or wider, within the bound.
A program may use at most 64 MiB of HBM per device.

v0:
```python
import jax
import jax.numpy as jnp
from jax import lax
from jax.sharding import PartitionSpec as P

DILATION_STEP = 8
epsilon = 1e-05


def with_halo(cells, sides, width):
    for axis, dim in sides:
        count = lax.axis_size(axis)
        ends = count - 1
        head = lax.slice_in_dim(cells, 0, width, axis=dim)
        tail = lax.slice_in_dim(cells, cells.shape[dim] - width, cells.shape[dim], axis=dim)
        cells = jnp.concatenate(
            [
                lax.ppermute(tail, axis, [(i, (i + 1) % count) for i in range(ends)]),
                cells,
                lax.ppermute(head, axis, [((i + 1) % count, i) for i in range(ends)]),
            ],
            axis=dim,
        )
    return cells


def dilated(receptive_region, weights):
    row_count = receptive_region.shape[1]
    col_count = receptive_region.shape[2]
    border_padded_input = with_halo(receptive_region, (("gx", 1), ("gy", 2)), DILATION_STEP)
    tap_sum_total = jnp.zeros((weights.shape[1], row_count, col_count), jnp.float32)
    for filter_tap_index in range(9):
        row_displacement = filter_tap_index // 3 * DILATION_STEP
        column_displacement = filter_tap_index % 3 * DILATION_STEP
        window = border_padded_input[
            :,
            row_displacement : row_displacement + row_count,
            column_displacement : column_displacement + col_count,
        ]
        tap_sum_total = tap_sum_total + jnp.einsum(
            "oc,crw->orw", weights[filter_tap_index], window, preferred_element_type=jnp.float32
        )
    return tap_sum_total


def normalized(tap_sum_total, gain, shift):
    cell_count = (
        tap_sum_total.shape[1] * tap_sum_total.shape[2] * lax.axis_size("gx") * lax.axis_size("gy")
    )
    first_sum, second_sum = lax.psum(
        (jnp.sum(tap_sum_total, axis=(1, 2)), jnp.sum(tap_sum_total * tap_sum_total, axis=(1, 2))),
        ("gx", "gy"),
    )
    average = first_sum / cell_count
    spread = second_sum / cell_count - average * average
    centred = tap_sum_total - average[:, None, None]
    factor = gain * lax.rsqrt(spread + epsilon)
    return centred * factor[:, None, None] + shift[:, None, None]


def body(residue_feats, pair_feats, w_row, w_col, first_taps, second_taps, norm_scale, norm_shift):
    col_count = pair_feats.shape[2]
    col_start = lax.axis_index("gy") * col_count
    row_part = jnp.dot(residue_feats, w_row, preferred_element_type=jnp.float32).astype(
        jnp.bfloat16
    )
    everyone = lax.all_gather(residue_feats, "gx", axis=0, tiled=True)
    col_feats = lax.dynamic_slice_in_dim(everyone, col_start, col_count, 0)
    col_part = jnp.dot(col_feats, w_col, preferred_element_type=jnp.float32).astype(jnp.bfloat16)
    block_in = (
        pair_feats.astype(jnp.float32)
        + row_part.T.astype(jnp.float32)[:, :, None]
        + col_part.T.astype(jnp.float32)[:, None, :]
    ).astype(jnp.bfloat16)
    first_conv = dilated(block_in, first_taps)
    activated = jax.nn.elu(normalized(first_conv, norm_scale[0], norm_shift[0])).astype(
        jnp.bfloat16
    )
    second_conv = dilated(activated, second_taps)
    block_out = jax.nn.elu(
        block_in.astype(jnp.float32) + normalized(second_conv, norm_scale[1], norm_shift[1])
    ).astype(jnp.bfloat16)
    whole_rows = lax.all_gather(block_out, "gy", axis=2, tiled=True)
    columns = lax.all_to_all(whole_rows, "gx", split_axis=2, concat_axis=1, tiled=True)
    flipped = lax.dynamic_slice_in_dim(columns, col_start, col_count, 1)
    mirrored = jnp.transpose(flipped, (0, 2, 1))
    return (0.5 * (block_out.astype(jnp.float32) + mirrored.astype(jnp.float32))).astype(
        jnp.bfloat16
    )


def solution(mesh):
    placed = (P(("grp", "gx"), None), P(None, ("grp", "gx"), "gy"), P(), P(), P(), P(), P(), P())
    return jax.shard_map(
        body, mesh=mesh, in_specs=placed, out_specs=P(None, ("grp", "gx"), "gy"), check_vma=False
    )
```

profile of v0, /device:TPU:0, one launch (start us, length us, event | category | flops | bytes accessed | tf_op | source)
XLA Modules:
  0.0 140.1 jit_solution(18333366935052121485)
XLA Ops:
  0.0 0.0 copy-start
  0.0 23.8 %all_gather.4 = bf16[256,256]{1,0:T(8,128)(2,1)S(1)} all-gather(bf16[16,256]{1,0:T(8,128)(2,1)} %param.8), channel_id=1, replica_groups=mesh['grp'=2,'gx'=16,'gy'=1] {'gx'}, dimensions={0}, use_global_device_ids=true | all-gather | bytes 139264 | tf_op jit(solution)/shard_map/all_gather | solution.py:67
  23.8 0.9 fusion.13
  24.7 0.2 fusion.12
  24.9 1.3 add_convert_fusion
  26.2 2.3 %collective-permute-start = (bf16[64,8,256]{2,0,1:T(8,128)(2,1)S(1)}, bf16[64,8,256]{2,0,1:T(8,128)(2,1)S(1)}, u32[]{:S(2)}, u32[]{:S(2)}) collective-permute-start(bf16[64,8,256]{2,0,1:T(8,128)(2,1)S(1)} %get-tuple-element.23), channel_id=1, source_target_pairs={{0,1},{1,2},{2,3},{3,4},{4,5},{5,6},{6,7},{7,8},{8,9},{9,10},{10,1... | collective-permute-start | bytes 786440 | tf_op jit(solution)/shard_map/ppermute | solution.py:18
  28.5 1.3 collective-permute-start.1
  29.8 0.0 copy-done.5
  29.8 0.3 fusion.62
  30.1 0.0 collective-permute-done
  30.1 1.8 %collective-permute-done.1 = bf16[64,8,256]{2,0,1:T(8,128)(2,1)S(1)} collective-permute-done((bf16[64,8,256]{2,0,1:T(8,128)(2,1)S(1)}, bf16[64,8,256]{2,0,1:T(8,128)(2,1)S(1)}, u32[]{:S(2)}, u32[]{:S(2)}) %collective-permute-start.1) | collective-permute-done | bytes 262176 | tf_op jit(solution)/shard_map/ppermute | solution.py:20
  31.9 0.1 pad_maximum_fusion.2
  32.1 0.3 fusion.93
  32.3 0.7 collective-permute-start.2
  33.0 0.7 collective-permute-start.3
  33.7 0.3 fusion.45
  34.0 0.3 fusion.36
  34.3 0.0 collective-permute-done.2
  34.3 0.0 collective-permute-done.3
  34.3 1.3 maximum_maximum_fusion
  35.6 0.4 fusion.43
  36.0 0.4 fusion.34
  36.4 0.3 fusion.41
  36.7 0.3 fusion.38
  36.9 0.4 fusion.11
  37.3 0.0 copy-start.4
  37.3 0.7 fusion.91
  38.0 0.0 copy-start.3
  38.0 33.9 %all-reduce.1 = (f32[64]{0:T(128)S(1)}, f32[64]{0:T(128)S(1)}) all-reduce(f32[64]{0:T(128)S(1)} %get-tuple-element.8, f32[64]{0:T(128)S(1)} %get-tuple-element.7), channel_id=1, replica_groups=mesh['grp'=2,'gx'=16,'gy'=1] {'gx','gy'}, use_global_device_ids=true, to_apply=%region_3.0 | all-reduce | flops 128 | bytes 1024 | tf_op jit(solution)/shard_map/psum | solution.py:50
  72.0 0.0 copy-done.4
  72.0 0.6 fusion.15
  72.6 1.3 collective-permute-start.4
  73.9 1.3 collective-permute-start.5
  75.2 0.3 fusion.52
  75.5 0.0 collective-permute-done.4
  75.5 1.8 %collective-permute-done.5 = bf16[64,8,256]{2,0,1:T(8,128)(2,1)S(1)} collective-permute-done((bf16[64,8,256]{2,0,1:T(8,128)(2,1)S(1)}, bf16[64,8,256]{2,0,1:T(8,128)(2,1)S(1)}, u32[]{:S(2)}, u32[]{:S(2)}) %collective-permute-start.5) | collective-permute-done | bytes 262176 | tf_op jit(solution)/shard_map/ppermute | solution.py:20
  77.4 0.1 pad_maximum_fusion.3
  77.5 0.3 fusion.92
  77.8 0.7 collective-permute-start.6
  78.5 0.7 collective-permute-start.7
  79.2 0.3 fusion.31
  79.4 0.3 fusion.22
  79.7 0.0 collective-permute-done.6
  79.7 0.0 collective-permute-done.7
  79.7 1.3 maximum_maximum_fusion.1
  81.0 0.4 fusion.29
  81.4 0.4 fusion.20
  81.8 0.3 fusion.27
  82.1 0.3 fusion.24
  82.3 0.4 fusion.5
  82.7 0.0 copy-start.1
  82.8 0.7 fusion.90
  83.4 31.5 %all-reduce = (f32[64]{0:T(128)S(1)}, f32[64]{0:T(128)S(1)}) all-reduce(f32[64]{0:T(128)S(1)} %get-tuple-element.6, f32[64]{0:T(128)S(1)} %get-tuple-element.5), channel_id=1, replica_groups=mesh['grp'=2,'gx'=16,'gy'=1] {'gx','gy'}, use_global_device_ids=true, to_apply=%region_7.8 | all-reduce | flops 128 | bytes 1024 | tf_op jit(solution)/shard_map/psum | solution.py:50
  115.0 0.7 fusion.17
  115.7 1.0 copy.18
  116.7 0.7 reshape.32
  117.4 16.9 %all_to_all.4 = bf16[16,2,8192]{2,1,0:T(2,128)(2,1)S(1)} all-to-all(bf16[16,2,8192]{2,1,0:T(2,128)(2,1)S(1)} %reshape.32), channel_id=1, replica_groups=mesh['grp'=2,'gx'=16,'gy'=1] {'gx'}, dimensions={0} | all-to-all | bytes 1048576 | tf_op jit(solution)/shard_map/all_to_all | solution.py:84
  134.3 0.7 reshape.33
  135.0 0.3 copy.19
  135.2 0.2 convert_bitcast_fusion
  135.5 0.2 copy.20
  135.7 2.0 %copy.21 = f32[64,256,16]{1,0,2:T(8,128)} copy(f32[64,256,16]{0,2,1:T(8,128)S(1)} %bitcast.109) | data formatting | bytes 2097152 | tf_op jit(solution)/shard_map/convert_element_type | solution.py:87
  137.6 1.4 fusion.19
  139.0 1.1 copy.22
  (11 shorter events, 0.1 us)
Async XLA Ops:
  0.0 24.7 %copy-start = (bf16[256,64]{0,1:T(8,128)(2,1)S(1)}, bf16[256,64]{0,1:T(8,128)(2,1)}, u32[]{:S(2)}) copy-start(bf16[256,64]{0,1:T(8,128)(2,1)} %param.11) | copy-start | bytes 98308
  0.0 29.8 %copy-start.5 = (f32[2,64]{1,0:T(2,128)S(1)}, f32[2,64]{1,0:T(2,128)}, u32[]{:S(2)}) copy-start(f32[2,64]{1,0:T(2,128)} %param.15) | copy-start | bytes 1540
  0.0 29.8 %copy-start.2 = (bf16[9,64,64]{2,1,0:T(8,128)(2,1)S(1)}, bf16[9,64,64]{2,1,0:T(8,128)(2,1)}, u32[]{:S(2)}) copy-start(bf16[9,64,64]{2,1,0:T(8,128)(2,1)} %param.12) | copy-start | bytes 221188
  26.2 3.9 %collective-permute-start = (bf16[64,8,256]{2,0,1:T(8,128)(2,1)S(1)}, bf16[64,8,256]{2,0,1:T(8,128)(2,1)S(1)}, u32[]{:S(2)}, u32[]{:S(2)}) collective-permute-start(bf16[64,8,256]{2,0,1:T(8,128)(2,1)S(1)} %get-tuple-element.23), channel_id=1, source_target_pairs={{0,1},{1,2},{2,3},{3,4},{4,5},{5,6},{6,7},{7,8},{8,9},{9,10},{10,1... | collective-permute-start | bytes 786440 | tf_op jit(solution)/shard_map/ppermute | solution.py:18
  28.5 3.4 %collective-permute-start.1 = (bf16[64,8,256]{2,0,1:T(8,128)(2,1)S(1)}, bf16[64,8,256]{2,0,1:T(8,128)(2,1)S(1)}, u32[]{:S(2)}, u32[]{:S(2)}) collective-permute-start(bf16[64,8,256]{2,0,1:T(8,128)(2,1)S(1)} %get-tuple-element.24), channel_id=1, source_target_pairs={{1,0},{2,1},{3,2},{4,3},{5,4},{6,5},{7,6},{8,7},{9,8},{10,9},{11,1... | collective-permute-start | bytes 786440 | tf_op jit(solution)/shard_map/ppermute | solution.py:20
  32.3 1.9 %collective-permute-start.2 = (bf16[64,32,8]{2,0,1:T(8,128)(2,1)S(1)}, bf16[64,32,8]{2,0,1:T(8,128)(2,1)S(1)}, u32[]{:S(2)}, u32[]{:S(2)}) collective-permute-start(bf16[64,32,8]{2,0,1:T(8,128)(2,1)S(1)} %get-tuple-element.19), channel_id=1, source_target_pairs={} | collective-permute-start | bytes 98312 | tf_op jit(solution)/shard_map/ppermute | solution.py:18
  33.0 1.3 collective-permute-start.3
  37.3 34.6 %copy-start.4 = (f32[2,64]{1,0:T(2,128)S(1)}, f32[2,64]{1,0:T(2,128)}, u32[]{:S(2)}) copy-start(f32[2,64]{1,0:T(2,128)} %param.14) | copy-start | bytes 1540
  38.0 37.2 %copy-start.3 = (bf16[9,64,64]{2,1,0:T(8,128)(2,1)S(1)}, bf16[9,64,64]{2,1,0:T(8,128)(2,1)}, u32[]{:S(2)}) copy-start(bf16[9,64,64]{2,1,0:T(8,128)(2,1)} %param.13) | copy-start | bytes 221188
  72.6 2.9 %collective-permute-start.4 = (bf16[64,8,256]{2,0,1:T(8,128)(2,1)S(1)}, bf16[64,8,256]{2,0,1:T(8,128)(2,1)S(1)}, u32[]{:S(2)}, u32[]{:S(2)}) collective-permute-start(bf16[64,8,256]{2,0,1:T(8,128)(2,1)S(1)} %get-tuple-element.21), channel_id=1, source_target_pairs={{0,1},{1,2},{2,3},{3,4},{4,5},{5,6},{6,7},{7,8},{8,9},{9,10},{10,1... | collective-permute-start | bytes 786440 | tf_op jit(solution)/shard_map/ppermute | solution.py:18
  73.9 3.4 %collective-permute-start.5 = (bf16[64,8,256]{2,0,1:T(8,128)(2,1)S(1)}, bf16[64,8,256]{2,0,1:T(8,128)(2,1)S(1)}, u32[]{:S(2)}, u32[]{:S(2)}) collective-permute-start(bf16[64,8,256]{2,0,1:T(8,128)(2,1)S(1)} %get-tuple-element.22), channel_id=1, source_target_pairs={{1,0},{2,1},{3,2},{4,3},{5,4},{6,5},{7,6},{8,7},{9,8},{10,9},{11,1... | collective-permute-start | bytes 786440 | tf_op jit(solution)/shard_map/ppermute | solution.py:20
  77.8 1.9 %collective-permute-start.6 = (bf16[64,32,8]{2,0,1:T(8,128)(2,1)S(1)}, bf16[64,32,8]{2,0,1:T(8,128)(2,1)S(1)}, u32[]{:S(2)}, u32[]{:S(2)}) collective-permute-start(bf16[64,32,8]{2,0,1:T(8,128)(2,1)S(1)} %get-tuple-element.15), channel_id=1, source_target_pairs={} | collective-permute-start | bytes 98312 | tf_op jit(solution)/shard_map/ppermute | solution.py:18
  78.5 1.3 collective-permute-start.7
  82.7 32.2 %copy-start.1 = (bf16[64,16,256]{2,1,0:T(8,128)(2,1)S(1)}, bf16[64,16,256]{2,1,0:T(8,128)(2,1)}, u32[]{:S(2)}) copy-start(bf16[64,16,256]{2,1,0:T(8,128)(2,1)} %param.9) | copy-start | bytes 1572868
where the time goes:
time: 141 us; the launch traced here: 140 us
  blocking collectives  106 us (75%)
  starting transfers between devices  8.9 us (6%)
  matrix products  7.38 us (5%)
  other arithmetic  7.08 us (5%)
  local copies, waits for them, and re-layouts  6.52 us (5%)
  waiting for transfers between devices  3.66 us (3%)
    psum x2, blocking collectives, normalized(): lax.psum((jnp.sum(tap_sum_total, axis=(1, 2)), jnp.sum(tap_sum_total * ta...  65.5 us
    all_gather x1, blocking collectives, body(): everyone = lax.all_gather(residue_feats, 'gx', axis=0, tiled=True)  23.8 us
    all_to_all x1, blocking collectives, body(): lax.all_to_all(whole_rows, 'gx', split_axis=2, concat_axis=1, tiled=True)  16.9 us
    dot_general x18, matrix products, dilated(): jnp.einsum('oc,crw->orw', weights[filter_tap_index], window, preferred_el...  6.34 us
    ppermute x4, starting transfers between devices, with_halo(): lax.ppermute(tail, axis, [(i, (i + 1) % count) for i in range(ends)])  4.94 us
    ppermute x4, starting transfers between devices, with_halo(): lax.ppermute(head, axis, [((i + 1) % count, i) for i in range(ends)])  3.96 us
    ppermute x4, waiting for transfers between devices, with_halo(): lax.ppermute(head, axis, [((i + 1) % count, i) for i in range(ends)])  3.65 us
    concatenate x4, other arithmetic, with_halo(): jnp.concatenate([lax.ppermute(tail, axis, [(i, (i + 1) % count) for i in...  2.87 us
  transfers between devices with their start and end apart: 8, of which 2 were waited for; matrix products, arithmetic and copies ran while one was open for 1% of the time, Pallas kernels for 0%

commit v1 on v0

--- a/solution.py
+++ b/solution.py
@@ -64,7 +64,21 @@
     row_part = jnp.dot(residue_feats, w_row, preferred_element_type=jnp.float32).astype(
         jnp.bfloat16
     )
-    everyone = lax.all_gather(residue_feats, "gx", axis=0, tiled=True)
+    ways, here, lap = (lax.axis_size("gx"), lax.axis_index("gx"), residue_feats.shape[0])
+    lengths = [n * ways if d == 0 else n for d, n in enumerate(residue_feats.shape)]
+    full = lax.dynamic_update_slice_in_dim(
+        jnp.zeros(lengths, residue_feats.dtype), residue_feats, here * lap, axis=0
+    )
+    going_up = going_down = residue_feats
+    for far in range(1, ways // 2 + 1):
+        going_up = lax.ppermute(going_up, "gx", [(d, (d + 1) % ways) for d in range(ways)])
+        full = lax.dynamic_update_slice_in_dim(full, going_up, (here - far) % ways * lap, axis=0)
+        if 2 * far < ways:
+            going_down = lax.ppermute(going_down, "gx", [(d, (d - 1) % ways) for d in range(ways)])
+            full = lax.dynamic_update_slice_in_dim(
+                full, going_down, (here + far) % ways * lap, axis=0
+            )
+    everyone = full
     col_feats = lax.dynamic_slice_in_dim(everyone, col_start, col_count, 0)
     col_part = jnp.dot(col_feats, w_col, preferred_element_type=jnp.float32).astype(jnp.bfloat16)
     block_in = (

time: 141 us -> 162 us (1.15)
  starting transfers between devices: 8.9 us -> 40.1 us
  blocking collectives: 106 us -> 80.7 us
  waiting for transfers between devices: 3.66 us -> 17.6 us
    ppermute x0 -> x15, starting transfers between devices: none -> 32 us  [the longest x7 31.5 us: body(): lax.ppermute(going_down, 'gx', [(d, (d - 1) % ways) for d in range(ways)])]
    all_gather x1 -> x0, blocking collectives: 23.8 us -> none  [body(): everyone = lax.all_gather(residue_feats, 'gx', axis=0, tiled=True)]
    ppermute x0 -> x15, waiting for transfers between devices: none -> 13.9 us  [the longest x8 13.7 us: body(): lax.ppermute(going_up, 'gx', [(d, (d + 1) % ways) for d in range(ways)])]
  transfers between devices with their start and end apart: 8 -> 23, of which waited for: 2 -> 9; matrix products, arithmetic and copies ran while one was open for 1% -> 3% of each run, Pallas kernels for 0% -> 0%
where the time goes in v1:
time: 162 us; the launch traced here: 161 us
  blocking collectives  80.7 us (50%)
  starting transfers between devices  40.1 us (25%)
  waiting for transfers between devices  17.6 us (11%)
  local copies, waits for them, and re-layouts  8.05 us (5%)
  matrix products  7.4 us (5%)
  other arithmetic  7.08 us (4%)
    psum x2, blocking collectives, normalized(): lax.psum((jnp.sum(tap_sum_total, axis=(1, 2)), jnp.sum(tap_sum_total * ta...  63.8 us
    ppermute x7, starting transfers between devices, body(): lax.ppermute(going_down, 'gx', [(d, (d - 1) % ways) for d in range(ways)])  31.5 us
    all_to_all x1, blocking collectives, body(): lax.all_to_all(whole_rows, 'gx', split_axis=2, concat_axis=1, tiled=True)  16.9 us
    ppermute x8, waiting for transfers between devices, body(): lax.ppermute(going_up, 'gx', [(d, (d + 1) % ways) for d in range(ways)])  13.7 us
    dot_general x18, matrix products, dilated(): jnp.einsum('oc,crw->orw', weights[filter_tap_index], window, preferred_el...  6.33 us
    ppermute x4, starting transfers between devices, with_halo(): lax.ppermute(tail, axis, [(i, (i + 1) % count) for i in range(ends)])  4.18 us
    ppermute x4, starting transfers between devices, with_halo(): lax.ppermute(head, axis, [((i + 1) % count, i) for i in range(ends)])  3.96 us
    ppermute x4, waiting for transfers between devices, with_halo(): lax.ppermute(head, axis, [((i + 1) % count, i) for i in range(ends)])  3.67 us
  transfers between devices with their start and end apart: 23, of which 9 were waited for; matrix products, arithmetic and copies ran while one was open for 3% of the time, Pallas kernels for 0%

profile of v1, /device:TPU:0, one launch (start us, length us, event | category | flops | bytes accessed | tf_op | source)
XLA Modules:
  0.0 161.4 jit_solution(11027126331277012322)
XLA Ops:
  0.0 0.5 collective-permute-start
  0.5 5.0 %collective-permute-start.1 = (bf16[16,256]{1,0:T(8,128)(2,1)}, bf16[16,256]{1,0:T(8,128)(2,1)S(1)}, u32[]{:S(2)}, u32[]{:S(2)}) collective-permute-start(bf16[16,256]{1,0:T(8,128)(2,1)} %param.8), channel_id=1, source_target_pairs={{0,15},{1,0},{2,1},{3,2},{4,3},{5,4},{6,5},{7,6},{8,7},{9,8},{10,9... | collective-permute-start | bytes 24584 | tf_op jit(solution)/shard_map/ppermute | solution.py:77
  5.5 0.9 fusion.14
  6.4 0.8 slice_bitcast_fusion
  7.2 0.7 constant_dynamic-update-slice_fusion.15
  7.9 4.4 %collective-permute-start.3 = (bf16[16,256]{1,0:T(8,128)(2,1)S(1)}, bf16[16,256]{1,0:T(8,128)(2,1)S(1)}, u32[]{:S(2)}, u32[]{:S(2)}) collective-permute-start(bf16[16,256]{1,0:T(8,128)(2,1)S(1)} %collective-permute-done.1), channel_id=1, source_target_pairs={{0,15},{1,0},{2,1},{3,2},{4,3},{5,4},{6,5},{7,6},{8,7},{9,8},{10,9... | collective-permute-start | bytes 24584 | tf_op jit(solution)/shard_map/ppermute | solution.py:77
  12.4 1.3 collective-permute-done.2
  13.7 4.4 %collective-permute-start.5 = (bf16[16,256]{1,0:T(8,128)(2,1)S(1)}, bf16[16,256]{1,0:T(8,128)(2,1)S(1)}, u32[]{:S(2)}, u32[]{:S(2)}) collective-permute-start(bf16[16,256]{1,0:T(8,128)(2,1)S(1)} %collective-permute-done.3), channel_id=1, source_target_pairs={{0,15},{1,0},{2,1},{3,2},{4,3},{5,4},{6,5},{7,6},{8,7},{9,8},{10,9... | collective-permute-start | bytes 24584 | tf_op jit(solution)/shard_map/ppermute | solution.py:77
  18.1 1.3 collective-permute-done.4
  19.5 4.4 %collective-permute-start.7 = (bf16[16,256]{1,0:T(8,128)(2,1)S(1)}, bf16[16,256]{1,0:T(8,128)(2,1)S(1)}, u32[]{:S(2)}, u32[]{:S(2)}) collective-permute-start(bf16[16,256]{1,0:T(8,128)(2,1)S(1)} %collective-permute-done.5), channel_id=1, source_target_pairs={{0,15},{1,0},{2,1},{3,2},{4,3},{5,4},{6,5},{7,6},{8,7},{9,8},{10,9... | collective-permute-start | bytes 24584 | tf_op jit(solution)/shard_map/ppermute | solution.py:77
  23.9 1.3 collective-permute-done.6
  25.3 4.4 %collective-permute-start.9 = (bf16[16,256]{1,0:T(8,128)(2,1)S(1)}, bf16[16,256]{1,0:T(8,128)(2,1)S(1)}, u32[]{:S(2)}, u32[]{:S(2)}) collective-permute-start(bf16[16,256]{1,0:T(8,128)(2,1)S(1)} %collective-permute-done.7), channel_id=1, source_target_pairs={{0,15},{1,0},{2,1},{3,2},{4,3},{5,4},{6,5},{7,6},{8,7},{9,8},{10,9... | collective-permute-start | bytes 24584 | tf_op jit(solution)/shard_map/ppermute | solution.py:77
  29.7 1.3 collective-permute-done.8
  31.1 4.4 %collective-permute-start.11 = (bf16[16,256]{1,0:T(8,128)(2,1)S(1)}, bf16[16,256]{1,0:T(8,128)(2,1)S(1)}, u32[]{:S(2)}, u32[]{:S(2)}) collective-permute-start(bf16[16,256]{1,0:T(8,128)(2,1)S(1)} %collective-permute-done.9), channel_id=1, source_target_pairs={{0,15},{1,0},{2,1},{3,2},{4,3},{5,4},{6,5},{7,6},{8,7},{9,8},{10,9... | collective-permute-start | bytes 24584 | tf_op jit(solution)/shard_map/ppermute | solution.py:77
  35.5 1.3 collective-permute-done.10
  36.8 4.4 %collective-permute-start.13 = (bf16[16,256]{1,0:T(8,128)(2,1)S(1)}, bf16[16,256]{1,0:T(8,128)(2,1)S(1)}, u32[]{:S(2)}, u32[]{:S(2)}) collective-permute-start(bf16[16,256]{1,0:T(8,128)(2,1)S(1)} %collective-permute-done.11), channel_id=1, source_target_pairs={{0,15},{1,0},{2,1},{3,2},{4,3},{5,4},{6,5},{7,6},{8,7},{9,8},{10,9... | collective-permute-start | bytes 24584 | tf_op jit(solution)/shard_map/ppermute | solution.py:77
  41.2 1.3 collective-permute-done.12
  42.6 5.7 %collective-permute-done.14 = bf16[16,256]{1,0:T(8,128)(2,1)S(1)} collective-permute-done((bf16[16,256]{1,0:T(8,128)(2,1)S(1)}, bf16[16,256]{1,0:T(8,128)(2,1)S(1)}, u32[]{:S(2)}, u32[]{:S(2)}) %collective-permute-start.14) | collective-permute-done | bytes 8224 | tf_op jit(solution)/shard_map/ppermute | solution.py:74
  48.5 1.3 add_convert_fusion
  49.8 1.3 collective-permute-start.15
  51.2 1.3 collective-permute-start.16
  52.5 0.3 fusion.63
  52.8 1.8 %collective-permute-done.16 = bf16[64,8,256]{2,0,1:T(8,128)(2,1)S(1)} collective-permute-done((bf16[64,8,256]{2,0,1:T(8,128)(2,1)S(1)}, bf16[64,8,256]{2,0,1:T(8,128)(2,1)S(1)}, u32[]{:S(2)}, u32[]{:S(2)}) %collective-permute-start.16) | collective-permute-done | bytes 262176 | tf_op jit(solution)/shard_map/ppermute | solution.py:20
  54.7 0.3 fusion.94
  55.0 0.7 collective-permute-start.17
  55.7 0.7 collective-permute-start.18
  56.4 0.3 fusion.46
  56.7 0.3 fusion.37
  57.0 1.3 maximum_maximum_fusion
  58.3 0.4 fusion.44
  58.7 0.4 fusion.35
  59.0 0.3 fusion.42
  59.3 0.3 fusion.39
  59.6 0.4 fusion.11
  60.0 0.7 fusion.92
  60.7 29.9 %all-reduce.1 = (f32[64]{0:T(128)S(1)}, f32[64]{0:T(128)S(1)}) all-reduce(f32[64]{0:T(128)S(1)} %get-tuple-element.8, f32[64]{0:T(128)S(1)} %get-tuple-element.7), channel_id=1, replica_groups=mesh['grp'=2,'gx'=16,'gy'=1] {'gx','gy'}, use_global_device_ids=true, to_apply=%region_3.4 | all-reduce | flops 128 | bytes 1024 | tf_op jit(solution)/shard_map/psum | solution.py:50
  90.6 0.6 fusion.16
  91.2 1.5 collective-permute-start.19
  92.8 1.3 collective-permute-start.20
  94.1 0.3 fusion.53
  94.3 1.8 %collective-permute-done.20 = bf16[64,8,256]{2,0,1:T(8,128)(2,1)S(1)} collective-permute-done((bf16[64,8,256]{2,0,1:T(8,128)(2,1)S(1)}, bf16[64,8,256]{2,0,1:T(8,128)(2,1)S(1)}, u32[]{:S(2)}, u32[]{:S(2)}) %collective-permute-start.20) | collective-permute-done | bytes 262176 | tf_op jit(solution)/shard_map/ppermute | solution.py:20
  96.3 0.3 fusion.93
  96.6 0.7 collective-permute-start.21
  97.3 0.7 collective-permute-start.22
  98.0 0.3 fusion.32
  98.3 0.3 fusion.23
  98.6 1.3 maximum_maximum_fusion.1
  99.9 0.4 fusion.30
  100.2 0.4 fusion.21
  100.6 0.3 fusion.28
  100.9 0.3 fusion.25
  101.2 0.4 fusion.5
  101.6 0.7 fusion.91
  102.3 33.9 %all-reduce = (f32[64]{0:T(128)S(1)}, f32[64]{0:T(128)S(1)}) all-reduce(f32[64]{0:T(128)S(1)} %get-tuple-element.6, f32[64]{0:T(128)S(1)} %get-tuple-element.5), channel_id=1, replica_groups=mesh['grp'=2,'gx'=16,'gy'=1] {'gx','gy'}, use_global_device_ids=true, to_apply=%region_7.8 | all-reduce | flops 128 | bytes 1024 | tf_op jit(solution)/shard_map/psum | solution.py:50
  136.2 0.7 fusion.18
  136.9 1.0 copy.18
  137.9 0.7 reshape.32
  138.6 16.9 %all_to_all.4 = bf16[16,2,8192]{2,1,0:T(2,128)(2,1)S(1)} all-to-all(bf16[16,2,8192]{2,1,0:T(2,128)(2,1)S(1)} %reshape.32), channel_id=1, replica_groups=mesh['grp'=2,'gx'=16,'gy'=1] {'gx'}, dimensions={0} | all-to-all | bytes 1048576 | tf_op jit(solution)/shard_map/all_to_all | solution.py:98
  155.5 0.7 reshape.33
  156.2 0.3 copy.19
  156.5 0.2 convert_bitcast_fusion
  156.9 2.0 %copy.21 = f32[64,256,16]{1,0,2:T(8,128)} copy(f32[64,256,16]{0,2,1:T(8,128)S(1)} %bitcast.111) | data formatting | bytes 2097152 | tf_op jit(solution)/shard_map/convert_element_type | solution.py:101
  158.9 1.4 fusion.20
  160.3 1.1 copy.22
  (55 shorter events, 1.0 us)
Async XLA Ops:
  0.0 48.3 %copy-start = (bf16[256,64]{0,1:T(8,128)(2,1)S(1)}, bf16[256,64]{0,1:T(8,128)(2,1)}, u32[]{:S(2)}) copy-start(bf16[256,64]{0,1:T(8,128)(2,1)} %param.11) | copy-start | bytes 98308
  0.0 7.9 %collective-permute-start = (bf16[16,256]{1,0:T(8,128)(2,1)}, bf16[16,256]{1,0:T(8,128)(2,1)S(1)}, u32[]{:S(2)}, u32[]{:S(2)}) collective-permute-start(bf16[16,256]{1,0:T(8,128)(2,1)} %param.8), channel_id=1, source_target_pairs={{0,1},{1,2},{2,3},{3,4},{4,5},{5,6},{6,7},{7,8},{8,9},{9,10},{10,1... | collective-permute-start | bytes 24584 | tf_op jit(solution)/shard_map/ppermute | solution.py:74
  0.5 7.4 %collective-permute-start.1 = (bf16[16,256]{1,0:T(8,128)(2,1)}, bf16[16,256]{1,0:T(8,128)(2,1)S(1)}, u32[]{:S(2)}, u32[]{:S(2)}) collective-permute-start(bf16[16,256]{1,0:T(8,128)(2,1)} %param.8), channel_id=1, source_target_pairs={{0,15},{1,0},{2,1},{3,2},{4,3},{5,4},{6,5},{7,6},{8,7},{9,8},{10,9... | collective-permute-start | bytes 24584 | tf_op jit(solution)/shard_map/ppermute | solution.py:77
  5.5 47.0 %copy-start.2 = (bf16[9,64,64]{2,1,0:T(8,128)(2,1)S(1)}, bf16[9,64,64]{2,1,0:T(8,128)(2,1)}, u32[]{:S(2)}) copy-start(bf16[9,64,64]{2,1,0:T(8,128)(2,1)} %param.12) | copy-start | bytes 221188
  7.9 5.8 %collective-permute-start.2 = (bf16[16,256]{1,0:T(8,128)(2,1)S(1)}, bf16[16,256]{1,0:T(8,128)(2,1)S(1)}, u32[]{:S(2)}, u32[]{:S(2)}) collective-permute-start(bf16[16,256]{1,0:T(8,128)(2,1)S(1)} %collective-permute-done), channel_id=1, source_target_pairs={{0,1},{1,2},{2,3},{3,4},{4,5},{5,6},{6,7},{7,8},{8,9},{9,10},{10,1... | collective-permute-start | bytes 24584 | tf_op jit(solution)/shard_map/ppermute | solution.py:74
  7.9 5.8 %collective-permute-start.3 = (bf16[16,256]{1,0:T(8,128)(2,1)S(1)}, bf16[16,256]{1,0:T(8,128)(2,1)S(1)}, u32[]{:S(2)}, u32[]{:S(2)}) collective-permute-start(bf16[16,256]{1,0:T(8,128)(2,1)S(1)} %collective-permute-done.1), channel_id=1, source_target_pairs={{0,15},{1,0},{2,1},{3,2},{4,3},{5,4},{6,5},{7,6},{8,7},{9,8},{10,9... | collective-permute-start | bytes 24584 | tf_op jit(solution)/shard_map/ppermute | solution.py:77
  13.7 5.8 %collective-permute-start.4 = (bf16[16,256]{1,0:T(8,128)(2,1)S(1)}, bf16[16,256]{1,0:T(8,128)(2,1)S(1)}, u32[]{:S(2)}, u32[]{:S(2)}) collective-permute-start(bf16[16,256]{1,0:T(8,128)(2,1)S(1)} %collective-permute-done.2), channel_id=1, source_target_pairs={{0,1},{1,2},{2,3},{3,4},{4,5},{5,6},{6,7},{7,8},{8,9},{9,10},{10,1... | collective-permute-start | bytes 24584 | tf_op jit(solution)/shard_map/ppermute | solution.py:74
  13.7 5.8 %collective-permute-start.5 = (bf16[16,256]{1,0:T(8,128)(2,1)S(1)}, bf16[16,256]{1,0:T(8,128)(2,1)S(1)}, u32[]{:S(2)}, u32[]{:S(2)}) collective-permute-start(bf16[16,256]{1,0:T(8,128)(2,1)S(1)} %collective-permute-done.3), channel_id=1, source_target_pairs={{0,15},{1,0},{2,1},{3,2},{4,3},{5,4},{6,5},{7,6},{8,7},{9,8},{10,9... | collective-permute-start | bytes 24584 | tf_op jit(solution)/shard_map/ppermute | solution.py:77
  19.5 5.8 %collective-permute-start.6 = (bf16[16,256]{1,0:T(8,128)(2,1)S(1)}, bf16[16,256]{1,0:T(8,128)(2,1)S(1)}, u32[]{:S(2)}, u32[]{:S(2)}) collective-permute-start(bf16[16,256]{1,0:T(8,128)(2,1)S(1)} %collective-permute-done.4), channel_id=1, source_target_pairs={{0,1},{1,2},{2,3},{3,4},{4,5},{5,6},{6,7},{7,8},{8,9},{9,10},{10,1... | collective-permute-start | bytes 24584 | tf_op jit(solution)/shard_map/ppermute | solution.py:74
  19.5 5.8 %collective-permute-start.7 = (bf16[16,256]{1,0:T(8,128)(2,1)S(1)}, bf16[16,256]{1,0:T(8,128)(2,1)S(1)}, u32[]{:S(2)}, u32[]{:S(2)}) collective-permute-start(bf16[16,256]{1,0:T(8,128)(2,1)S(1)} %collective-permute-done.5), channel_id=1, source_target_pairs={{0,15},{1,0},{2,1},{3,2},{4,3},{5,4},{6,5},{7,6},{8,7},{9,8},{10,9... | collective-permute-start | bytes 24584 | tf_op jit(solution)/shard_map/ppermute | solution.py:77
  25.2 5.8 %collective-permute-start.8 = (bf16[16,256]{1,0:T(8,128)(2,1)S(1)}, bf16[16,256]{1,0:T(8,128)(2,1)S(1)}, u32[]{:S(2)}, u32[]{:S(2)}) collective-permute-start(bf16[16,256]{1,0:T(8,128)(2,1)S(1)} %collective-permute-done.6), channel_id=1, source_target_pairs={{0,1},{1,2},{2,3},{3,4},{4,5},{5,6},{6,7},{7,8},{8,9},{9,10},{10,1... | collective-permute-start | bytes 24584 | tf_op jit(solution)/shard_map/ppermute | solution.py:74
  25.3 5.8 %collective-permute-start.9 = (bf16[16,256]{1,0:T(8,128)(2,1)S(1)}, bf16[16,256]{1,0:T(8,128)(2,1)S(1)}, u32[]{:S(2)}, u32[]{:S(2)}) collective-permute-start(bf16[16,256]{1,0:T(8,128)(2,1)S(1)} %collective-permute-done.7), channel_id=1, source_target_pairs={{0,15},{1,0},{2,1},{3,2},{4,3},{5,4},{6,5},{7,6},{8,7},{9,8},{10,9... | collective-permute-start | bytes 24584 | tf_op jit(solution)/shard_map/ppermute | solution.py:77
  31.0 5.8 %collective-permute-start.10 = (bf16[16,256]{1,0:T(8,128)(2,1)S(1)}, bf16[16,256]{1,0:T(8,128)(2,1)S(1)}, u32[]{:S(2)}, u32[]{:S(2)}) collective-permute-start(bf16[16,256]{1,0:T(8,128)(2,1)S(1)} %collective-permute-done.8), channel_id=1, source_target_pairs={{0,1},{1,2},{2,3},{3,4},{4,5},{5,6},{6,7},{7,8},{8,9},{9,10},{10,1... | collective-permute-start | bytes 24584 | tf_op jit(solution)/shard_map/ppermute | solution.py:74
  31.1 5.8 %collective-permute-start.11 = (bf16[16,256]{1,0:T(8,128)(2,1)S(1)}, bf16[16,256]{1,0:T(8,128)(2,1)S(1)}, u32[]{:S(2)}, u32[]{:S(2)}) collective-permute-start(bf16[16,256]{1,0:T(8,128)(2,1)S(1)} %collective-permute-done.9), channel_id=1, source_target_pairs={{0,15},{1,0},{2,1},{3,2},{4,3},{5,4},{6,5},{7,6},{8,7},{9,8},{10,9... | collective-permute-start | bytes 24584 | tf_op jit(solution)/shard_map/ppermute | solution.py:77
  36.8 5.8 %collective-permute-start.12 = (bf16[16,256]{1,0:T(8,128)(2,1)S(1)}, bf16[16,256]{1,0:T(8,128)(2,1)S(1)}, u32[]{:S(2)}, u32[]{:S(2)}) collective-permute-start(bf16[16,256]{1,0:T(8,128)(2,1)S(1)} %collective-permute-done.10), channel_id=1, source_target_pairs={{0,1},{1,2},{2,3},{3,4},{4,5},{5,6},{6,7},{7,8},{8,9},{9,10},{10,1... | collective-permute-start | bytes 24584 | tf_op jit(solution)/shard_map/ppermute | solution.py:74
  36.8 5.8 %collective-permute-start.13 = (bf16[16,256]{1,0:T(8,128)(2,1)S(1)}, bf16[16,256]{1,0:T(8,128)(2,1)S(1)}, u32[]{:S(2)}, u32[]{:S(2)}) collective-permute-start(bf16[16,256]{1,0:T(8,128)(2,1)S(1)} %collective-permute-done.11), channel_id=1, source_target_pairs={{0,15},{1,0},{2,1},{3,2},{4,3},{5,4},{6,5},{7,6},{8,7},{9,8},{10,9... | collective-permute-start | bytes 24584 | tf_op jit(solution)/shard_map/ppermute | solution.py:77
  42.6 5.8 %collective-permute-start.14 = (bf16[16,256]{1,0:T(8,128)(2,1)S(1)}, bf16[16,256]{1,0:T(8,128)(2,1)S(1)}, u32[]{:S(2)}, u32[]{:S(2)}) collective-permute-start(bf16[16,256]{1,0:T(8,128)(2,1)S(1)} %collective-permute-done.12), channel_id=1, source_target_pairs={{0,1},{1,2},{2,3},{3,4},{4,5},{5,6},{6,7},{7,8},{8,9},{9,10},{10,1... | collective-permute-start | bytes 24584 | tf_op jit(solution)/shard_map/ppermute | solution.py:74
  49.8 2.9 %collective-permute-start.15 = (bf16[64,8,256]{2,0,1:T(8,128)(2,1)S(1)}, bf16[64,8,256]{2,0,1:T(8,128)(2,1)S(1)}, u32[]{:S(2)}, u32[]{:S(2)}) collective-permute-start(bf16[64,8,256]{2,0,1:T(8,128)(2,1)S(1)} %get-tuple-element.23), channel_id=1, source_target_pairs={{0,1},{1,2},{2,3},{3,4},{4,5},{5,6},{6,7},{7,8},{8,9},{9,10},{10,1... | collective-permute-start | bytes 786440 | tf_op jit(solution)/shard_map/ppermute | solution.py:18
  51.2 3.4 %collective-permute-start.16 = (bf16[64,8,256]{2,0,1:T(8,128)(2,1)S(1)}, bf16[64,8,256]{2,0,1:T(8,128)(2,1)S(1)}, u32[]{:S(2)}, u32[]{:S(2)}) collective-permute-start(bf16[64,8,256]{2,0,1:T(8,128)(2,1)S(1)} %get-tuple-element.24), channel_id=1, source_target_pairs={{1,0},{2,1},{3,2},{4,3},{5,4},{6,5},{7,6},{8,7},{9,8},{10,9},{11,1... | collective-permute-start | bytes 786440 | tf_op jit(solution)/shard_map/ppermute | solution.py:20
  55.0 1.9 %collective-permute-start.17 = (bf16[64,32,8]{2,0,1:T(8,128)(2,1)S(1)}, bf16[64,32,8]{2,0,1:T(8,128)(2,1)S(1)}, u32[]{:S(2)}, u32[]{:S(2)}) collective-permute-start(bf16[64,32,8]{2,0,1:T(8,128)(2,1)S(1)} %get-tuple-element.19), channel_id=1, source_target_pairs={} | collective-permute-start | bytes 98312 | tf_op jit(solution)/shard_map/ppermute | solution.py:18
  55.7 1.3 collective-permute-start.18
  60.0 30.6 %copy-start.4 = (f32[2,64]{1,0:T(2,128)S(1)}, f32[2,64]{1,0:T(2,128)}, u32[]{:S(2)}) copy-start(f32[2,64]{1,0:T(2,128)} %param.14) | copy-start | bytes 1540
  60.7 33.4 %copy-start.3 = (bf16[9,64,64]{2,1,0:T(8,128)(2,1)S(1)}, bf16[9,64,64]{2,1,0:T(8,128)(2,1)}, u32[]{:S(2)}) copy-start(bf16[9,64,64]{2,1,0:T(8,128)(2,1)} %param.13) | copy-start | bytes 221188
  91.2 3.1 %collective-permute-start.19 = (bf16[64,8,256]{2,0,1:T(8,128)(2,1)S(1)}, bf16[64,8,256]{2,0,1:T(8,128)(2,1)S(1)}, u32[]{:S(2)}, u32[]{:S(2)}) collective-permute-start(bf16[64,8,256]{2,0,1:T(8,128)(2,1)S(1)} %get-tuple-element.21), channel_id=1, source_target_pairs={{0,1},{1,2},{2,3},{3,4},{4,5},{5,6},{6,7},{7,8},{8,9},{9,10},{10,1... | collective-permute-start | bytes 786440 | tf_op jit(solution)/shard_map/ppermute | solution.py:18
  92.8 3.4 %collective-permute-start.20 = (bf16[64,8,256]{2,0,1:T(8,128)(2,1)S(1)}, bf16[64,8,256]{2,0,1:T(8,128)(2,1)S(1)}, u32[]{:S(2)}, u32[]{:S(2)}) collective-permute-start(bf16[64,8,256]{2,0,1:T(8,128)(2,1)S(1)} %get-tuple-element.22), channel_id=1, source_target_pairs={{1,0},{2,1},{3,2},{4,3},{5,4},{6,5},{7,6},{8,7},{9,8},{10,9},{11,1... | collective-permute-start | bytes 786440 | tf_op jit(solution)/shard_map/ppermute | solution.py:20
  96.6 1.9 %collective-permute-start.21 = (bf16[64,32,8]{2,0,1:T(8,128)(2,1)S(1)}, bf16[64,32,8]{2,0,1:T(8,128)(2,1)S(1)}, u32[]{:S(2)}, u32[]{:S(2)}) collective-permute-start(bf16[64,32,8]{2,0,1:T(8,128)(2,1)S(1)} %get-tuple-element.15), channel_id=1, source_target_pairs={} | collective-permute-start | bytes 98312 | tf_op jit(solution)/shard_map/ppermute | solution.py:18
  97.3 1.3 collective-permute-start.22
  101.6 34.6 %copy-start.1 = (bf16[64,16,256]{2,1,0:T(8,128)(2,1)S(1)}, bf16[64,16,256]{2,1,0:T(8,128)(2,1)}, u32[]{:S(2)}) copy-start(bf16[64,16,256]{2,1,0:T(8,128)(2,1)} %param.9) | copy-start | bytes 1572868
